TPU v7x, 32 devices: a whole 2x2x4 slice. The times are simulated.
32 devices in a mesh: front: 8 (over y, x, core), sub: 4 (over z).
Axes of the slice: x: 2, y: 2, z: 4, core: 2. Of those that a mesh axis runs over, the one named last changes fastest.
Arguments:
- row_values: float32 [4096, 1024], P(('front', 'sub')), may hold values from -0.12 to 0.12
- front_of_row: int32 [4096, 1], P(('front', 'sub')), may hold values from 0 to 7; in each aligned block of 128 rows (0 to 127, 128 to 255, ...) at most 32 rows name the same one
- child_factors: float32 [16, 512, 512], P('front', 'sub'), as said below
- child_columns: int32 [16, 512], P('front'), may hold values from 0 to 1023, as said below
- damping: float32 [8, 1024], P('front'), may hold values from 0.5 to 2
Outputs:
- front_factor: float32 [8, 1024, 1024], P('front', 'sub')
Inputs may be any that keep to these rules, and one draw needn't show every extreme that they name: `front_of_row`: among the 128 rows of one device, at most 32 name the same front, and some device's block reaches this bound. `child_factors`: each block is upper triangular with a positive diagonal. `child_columns`: each row names 512 distinct columns.
All inputs are finite; a program needn't handle non-finite values.
Results may differ from a plain program's by a relative error of at most 0.0003.
Values sent between devices are 32-bit elements; how exact they have to be, the bound alone decides.
A program may use at most 64 MiB of HBM per device.

v0:
```python
import jax
import jax.numpy as jnp
from jax import lax
from jax.sharding import PartitionSpec as P

HIGHEST = lax.Precision.HIGHEST


def cross_product(left_cols, right_cols):
    return lax.dot_general(
        left_cols,
        right_cols,
        (((0,), (0,)), ((), ())),
        precision=HIGHEST,
        preferred_element_type=jnp.float32,
    )


def local(row_values, front_of_row, child_factors, child_columns, damping):
    fronts = lax.axis_size("front")
    rows_held, front_width = row_values.shape
    capacity = 2 * rows_held // fronts
    destination = front_of_row[:, 0]
    onehot = (destination[:, None] == jnp.arange(fronts, dtype=jnp.int32)[None, :]).astype(
        jnp.int32
    )
    position = jnp.sum((jnp.cumsum(onehot, axis=0) - onehot) * onehot, axis=1)
    slot_of = destination * capacity + position
    source = (
        jnp.full((fronts * capacity,), rows_held, jnp.int32)
        .at[slot_of]
        .set(jnp.arange(rows_held, dtype=jnp.int32))
    )
    padded = jnp.concatenate([row_values, jnp.zeros((1, front_width), row_values.dtype)], axis=0)
    outgoing = padded[source]
    received = lax.all_to_all(outgoing, "front", split_axis=0, concat_axis=0, tiled=True)
    columns = jnp.arange(front_width, dtype=jnp.int32)
    spread = (child_columns[:, :, None] == columns[None, None, :]).astype(jnp.float32)
    placed = jnp.einsum(
        "jrc,jcf->jrf", child_factors, spread, precision=HIGHEST, preferred_element_type=jnp.float32
    )
    stacked = jnp.concatenate([placed.reshape(-1, front_width), received], axis=0)
    sub_count = lax.axis_size("sub")
    block_rows = front_width // sub_count
    own_index = lax.axis_index("sub")
    weight = damping[0]
    summed_gram = lax.psum(cross_product(stacked, stacked), "sub")
    summed_gram = summed_gram + jnp.diag(weight * weight)
    full_factor = jnp.linalg.cholesky(summed_gram).T
    own_rows = lax.dynamic_slice_in_dim(full_factor, own_index * block_rows, block_rows, 0)
    return own_rows[None]


def solution(mesh):
    in_specs = (
        P(("front", "sub"), None),
        P(("front", "sub"), None),
        P("front", "sub", None),
        P("front", None),
        P("front", None),
    )
    out_specs = P("front", "sub", None)
    return jax.shard_map(local, mesh=mesh, in_specs=in_specs, out_specs=out_specs, check_vma=False)
```

profile of v0, /device:TPU:0, one launch (start us, length us, event | category | flops | bytes accessed | tf_op | source)
XLA Modules:
  0.0 432.0 jit_solution(13834568773688344293)
XLA Ops:
  13.1 5.2 %all-to-all-start = ((f32[8,32,1024]{2,1,0:T(8,128)}), f32[8,32,1024]{2,1,0:T(8,128)S(1)}, u32[]{:S(2)}, u32[]{:S(2)}) async-start(f32[8,32,1024]{2,1,0:T(8,128)} %bitcast.5), calls=%async_computation | async-start | bytes 2097152 | tf_op jit(solution)/shard_map/all_to_all | solution.py:36
  20.0 13.7 %all-to-all-done = f32[8,32,1024]{2,1,0:T(8,128)S(1)} async-done(((f32[8,32,1024]{2,1,0:T(8,128)}), f32[8,32,1024]{2,1,0:T(8,128)S(1)}, u32[]{:S(2)}, u32[]{:S(2)}) %all-to-all-start) | async-done | bytes 1048608 | tf_op jit(solution)/shard_map/all_to_all | solution.py:36
  33.7 8.4 %fusion.2 = f32[1024,1024]{0,1:T(8,128)} fusion(f32[256,1024]{1,0:T(8,128)S(1)} %bitcast.58, f32[256,1024]{1,0:T(8,128)S(1)} %bitcast.63), kind=kOutput, calls=%fused_computation.8 | convolution fusion | flops 6442975232 | bytes 6291456 | tf_op jit(solution)/shard_map/dot_general | solution.py:10
  42.9 153.9 %all-reduce.4.cloned.1.call-done = f32[1024,1024]{0,1:T(8,128)} async-done(((f32[1024,1024]{0,1:T(8,128)}), f32[1024,1024]{0,1:T(8,128)}) %all-reduce.4.cloned.1.call-update) | async-done | bytes 4194320 | tf_op jit(solution)/shard_map/psum | solution.py:47
  196.7 4.8 %select_add_fusion = f32[1024,1024]{0,1:T(8,128)} fusion(f32[1024,1024]{0,1:T(8,128)} %all-reduce.4.cloned.1.call-done, f32[1024]{0:T(1024)S(1)} %bitcast.59), kind=kLoop, calls=%fused_computation.4 | loop fusion | flops 3145728 | bytes 8392704 | tf_op jit(solution)/shard_map/add | solution.py:48
  201.6 5.5 %copy.7 = f32[1024,1024]{1,0:T(8,128)} copy(f32[1024,1024]{0,1:T(8,128)} %select_add_fusion) | data formatting | bytes 8388608 | tf_op jit(solution)/shard_map/add | solution.py:48
  207.1 4.4 %fusion = f32[1024,1024]{1,0:T(8,128)S(1)} fusion(f32[1024,1024]{1,0:T(8,128)} %copy.7, f32[1024,1024]{0,1:T(8,128)} %all-reduce.4.cloned.1.call-done, f32[1024]{0:T(1024)S(1)} %bitcast.60), kind=kLoop, calls=%fused_computation.3 | loop fusion | flops 5242880 | bytes 12587008 | tf_op jit(solution)/shard_map/jit(cholesky)/div | solution.py:49
  213.5 11.7 %cholesky.224 = f32[128,128]{1,0:T(8,128)S(1)} custom-call(f32[128,128]{1,0:T(8,128)S(1)} %cholesky.580), custom_call_target="Cholesky" | custom-call | tf_op jit(solution)/shard_map/jit(cholesky)/cholesky | solution.py:49
  225.4 9.8 %custom-call.59 = f32[1,128,128]{1,2,0:T(8,128)S(1)} custom-call(f32[1,128,128]{2,1,0:T(8,128)S(1)} %get-tuple-element.18), custom_call_target="InvertDiagBlocksLowerTriangular" | custom-call | tf_op jit(solution)/shard_map/jit(cholesky)/cholesky | solution.py:49
  238.5 11.7 %cholesky.245 = f32[128,128]{1,0:T(8,128)S(1)} custom-call(f32[128,128]{1,0:T(8,128)S(1)} %cholesky.584), custom_call_target="Cholesky" | custom-call | tf_op jit(solution)/shard_map/jit(cholesky)/cholesky | solution.py:49
  253.2 9.8 %custom-call.60 = f32[1,128,128]{1,2,0:T(8,128)S(1)} custom-call(f32[1,128,128]{2,1,0:T(8,128)S(1)} %get-tuple-element.16), custom_call_target="InvertDiagBlocksLowerTriangular" | custom-call | tf_op jit(solution)/shard_map/jit(cholesky)/cholesky | solution.py:49
  268.5 11.7 %cholesky.469 = f32[128,128]{1,0:T(8,128)S(1)} custom-call(f32[128,128]{1,0:T(8,128)S(1)} %cholesky.589), custom_call_target="Cholesky" | custom-call | tf_op jit(solution)/shard_map/jit(cholesky)/cholesky | solution.py:49
  281.0 9.8 %custom-call.61 = f32[1,128,128]{1,2,0:T(8,128)S(1)} custom-call(f32[1,128,128]{2,1,0:T(8,128)S(1)} %get-tuple-element.14), custom_call_target="InvertDiagBlocksLowerTriangular" | custom-call | tf_op jit(solution)/shard_map/jit(cholesky)/cholesky | solution.py:49
  292.1 3.3 convolution_subtract_fusion.2
  295.4 11.7 %cholesky.488 = f32[128,128]{1,0:T(8,128)S(1)} custom-call(f32[128,128]{1,0:T(8,128)S(1)} %cholesky.594), custom_call_target="Cholesky" | custom-call | tf_op jit(solution)/shard_map/jit(cholesky)/cholesky | solution.py:49
  307.9 9.8 %custom-call.62 = f32[1,128,128]{1,2,0:T(8,128)S(1)} custom-call(f32[1,128,128]{2,1,0:T(8,128)S(1)} %get-tuple-element.12), custom_call_target="InvertDiagBlocksLowerTriangular" | custom-call | tf_op jit(solution)/shard_map/jit(cholesky)/cholesky | solution.py:49
  318.8 3.1 convolution_subtract_fusion.3
  322.0 11.9 %cholesky.507 = f32[128,128]{1,0:T(8,128)S(1)} custom-call(f32[128,128]{1,0:T(8,128)S(1)} %cholesky.599), custom_call_target="Cholesky" | custom-call | tf_op jit(solution)/shard_map/jit(cholesky)/cholesky | solution.py:49
  334.7 9.8 %custom-call.63 = f32[1,128,128]{1,2,0:T(8,128)S(1)} custom-call(f32[1,128,128]{2,1,0:T(8,128)S(1)} %get-tuple-element.10), custom_call_target="InvertDiagBlocksLowerTriangular" | custom-call | tf_op jit(solution)/shard_map/jit(cholesky)/cholesky | solution.py:49
  348.7 11.7 %cholesky.527 = f32[128,128]{1,0:T(8,128)S(1)} custom-call(f32[128,128]{1,0:T(8,128)S(1)} %cholesky.604), custom_call_target="Cholesky" | custom-call | tf_op jit(solution)/shard_map/jit(cholesky)/cholesky | solution.py:49
  361.2 9.8 %custom-call.64 = f32[1,128,128]{1,2,0:T(8,128)S(1)} custom-call(f32[1,128,128]{2,1,0:T(8,128)S(1)} %get-tuple-element.8), custom_call_target="InvertDiagBlocksLowerTriangular" | custom-call | tf_op jit(solution)/shard_map/jit(cholesky)/cholesky | solution.py:49
  374.9 11.7 %cholesky.547 = f32[128,128]{1,0:T(8,128)S(1)} custom-call(f32[128,128]{1,0:T(8,128)S(1)} %cholesky.609), custom_call_target="Cholesky" | custom-call | tf_op jit(solution)/shard_map/jit(cholesky)/cholesky | solution.py:49
  387.4 9.8 %custom-call.65 = f32[1,128,128]{1,2,0:T(8,128)S(1)} custom-call(f32[1,128,128]{2,1,0:T(8,128)S(1)} %get-tuple-element.6), custom_call_target="InvertDiagBlocksLowerTriangular" | custom-call | tf_op jit(solution)/shard_map/jit(cholesky)/cholesky | solution.py:49
  400.2 11.7 %cholesky.565 = f32[128,128]{1,0:T(8,128)S(1)} custom-call(f32[128,128]{1,0:T(8,128)S(1)} %convolution_subtract_fusion.6), custom_call_target="Cholesky" | custom-call | tf_op jit(solution)/shard_map/jit(cholesky)/cholesky | solution.py:49
  (75 shorter events, 47.5 us)
Async XLA Ops:
  6.5 11.9 %copy-start = (f32[2,128,512]{2,1,0:T(8,128)S(1)}, f32[2,128,512]{2,1,0:T(8,128)}, u32[]{:S(2)}) copy-start(f32[2,128,512]{2,1,0:T(8,128)} %param.7) | copy-start | bytes 1572868
  11.1 7.3 %copy-start.3 = (s32[2,512]{1,0:T(2,128)S(1)}, s32[2,512]{1,0:T(2,128)}, u32[]{:S(2)}) copy-start(s32[2,512]{1,0:T(2,128)} %param.8) | copy-start | bytes 12292
  13.1 20.6 %all-to-all-start = ((f32[8,32,1024]{2,1,0:T(8,128)}), f32[8,32,1024]{2,1,0:T(8,128)S(1)}, u32[]{:S(2)}, u32[]{:S(2)}) async-start(f32[8,32,1024]{2,1,0:T(8,128)} %bitcast.5), calls=%async_computation | async-start | bytes 2097152 | tf_op jit(solution)/shard_map/all_to_all | solution.py:36
  18.3 178.4 %all-reduce.4.cloned.1.call-start = ((), (), s32[]{:S(2)}) async-start(), calls=%async_computation.1 | async-start | bytes 8388608 | tf_op jit(solution)/shard_map/psum | solution.py:47
  42.2 0.7 copy-start.2
  211.6 1.9 copy-start.1
Sparse Core Ops, SparseCore 0:
  42.3 154.3 all-reduce.3
where the time goes:
time: 438 us; the launch traced here: 432 us
  other arithmetic  182 us (42%)
  waiting for transfers between devices  168 us (38%)
  matrix products  37.1 us (8%)
  local copies, waits for them, and re-layouts  21 us (5%)
  between operations  19.5 us (4%)
  starting transfers between devices  5.24 us (1%)
    another operation x30, other arithmetic, local(): full_factor = jnp.linalg.cholesky(summed_gram).T  167 us
    psum x1, waiting for transfers between devices, local(): summed_gram = lax.psum(cross_product(stacked, stacked), 'sub')  154 us
    another operation x14, matrix products, local(): full_factor = jnp.linalg.cholesky(summed_gram).T  27 us
    all_to_all x1, waiting for transfers between devices, local(): lax.all_to_all(outgoing, 'front', split_axis=0, concat_axis=0, tiled=True)  13.7 us
    another operation x25, local copies, waits for them, and re-layouts, local(): full_factor = jnp.linalg.cholesky(summed_gram).T  8.78 us
  transfers between devices with their start and end apart: 2, of which 2 were waited for; matrix products, arithmetic and copies ran while one was open for 0% of the time, Pallas kernels for 0%

commit v1 on v0

--- a/solution.py
+++ b/solution.py
@@ -1,9 +1,19 @@
+import functools
 import jax
 import jax.numpy as jnp
 from jax import lax
 from jax.sharding import PartitionSpec as P
 
 HIGHEST = lax.Precision.HIGHEST
+
+
+def create_slot(u, dev_axis):
+    b_now = lax.all_gather(u, dev_axis)
+    carry_out = jnp.sum(b_now, 0)
+    return carry_out
+
+
+sections_lay = functools.partial(create_slot, dev_axis="sub")
 
 
 def cross_product(left_cols, right_cols):
@@ -44,7 +54,7 @@
     block_rows = front_width // sub_count
     own_index = lax.axis_index("sub")
     weight = damping[0]
-    summed_gram = lax.psum(cross_product(stacked, stacked), "sub")
+    summed_gram = sections_lay(cross_product(stacked, stacked))
     summed_gram = summed_gram + jnp.diag(weight * weight)
     full_factor = jnp.linalg.cholesky(summed_gram).T
     own_rows = lax.dynamic_slice_in_dim(full_factor, own_index * block_rows, block_rows, 0)

time: 438 us -> 571 us (1.30)
  waiting for transfers between devices: 168 us -> 299 us
  other arithmetic: 182 us -> 191 us
    all_gather x0 -> x1, waiting for transfers between devices: none -> 286 us  [create_slot(): b_now = lax.all_gather(u, dev_axis)]
    psum x1 -> x0, waiting for transfers between devices: 154 us -> none  [local(): summed_gram = lax.psum(cross_product(stacked, stacked), 'sub')]
    reduce_sum x0 -> x1, other arithmetic: none -> 10.3 us  [create_slot(): carry_out = jnp.sum(b_now, 0)]
    another operation x25 -> x8, local copies, waits for them, and re-layouts: 8.78 us -> 2.55 us  [local(): full_factor = jnp.linalg.cholesky(summed_gram).T]
where the time goes in v1:
time: 571 us; the launch traced here: 564 us
  waiting for transfers between devices  299 us (52%)
  other arithmetic  191 us (33%)
  matrix products  33 us (6%)
  between operations  18.9 us (3%)
  local copies, waits for them, and re-layouts  16.1 us (3%)
    all_gather x1, waiting for transfers between devices, create_slot(): b_now = lax.all_gather(u, dev_axis)  286 us
    another operation x30, other arithmetic, local(): full_factor = jnp.linalg.cholesky(summed_gram).T  172 us
    another operation x14, matrix products, local(): full_factor = jnp.linalg.cholesky(summed_gram).T  23.1 us
    all_to_all x1, waiting for transfers between devices, local(): lax.all_to_all(outgoing, 'front', split_axis=0, concat_axis=0, tiled=True)  13.7 us
  transfers between devices with their start and end apart: 2, of which 2 were waited for; matrix products, arithmetic and copies ran while one was open for 0% of the time, Pallas kernels for 0%

profile of v1, /device:TPU:0, one launch (start us, length us, event | category | flops | bytes accessed | tf_op | source)
XLA Modules:
  0.0 563.5 jit_solution(5917740742007001049)
XLA Ops:
  13.1 5.2 all-to-all-start
  20.0 13.7 %all-to-all-done = f32[8,32,1024]{2,1,0:T(8,128)S(1)} async-done(((f32[8,32,1024]{2,1,0:T(8,128)}), f32[8,32,1024]{2,1,0:T(8,128)S(1)}, u32[]{:S(2)}, u32[]{:S(2)}) %all-to-all-start) | async-done | bytes 1048608 | tf_op jit(solution)/shard_map/all_to_all | solution.py:46
  33.7 8.3 %fusion.1 = f32[1024,1024]{1,0:T(8,128)} fusion(f32[256,1024]{1,0:T(8,128)S(1)} %bitcast.60, f32[256,1024]{1,0:T(8,128)S(1)} %bitcast.64), kind=kOutput, calls=%fused_computation.7 | convolution fusion | flops 6442975232 | bytes 6291456 | tf_op jit(solution)/shard_map/dot_general | solution.py:20
  42.7 285.6 %all-gather.3.cloned.1.call-done = f32[4096,1024]{1,0:T(8,128)} async-done(((f32[1024,1024]{1,0:T(8,128)}), f32[4096,1024]{1,0:T(8,128)}) %all-gather.3.cloned.1.call-update) | async-done | bytes 16777232 | tf_op jit(solution)/shard_map/all_gather | solution.py:11
  328.4 10.3 %reduce_sum.24 = f32[1024,1024]{1,0:T(8,128)} reduce(f32[4,1024,1024]{2,1,0:T(8,128)} %bitcast.59, f32[]{:T(128)} %constant.277.clone.1), dimensions={0}, to_apply=%region_3.4 | reduce | flops 3145728 | bytes 20971524 | tf_op jit(solution)/shard_map/reduce_sum | solution.py:12
  338.7 5.5 copy.6
  344.2 4.5 add_multiply_fusion
  350.7 11.7 %cholesky.224 = f32[128,128]{1,0:T(8,128)S(1)} custom-call(f32[128,128]{1,0:T(8,128)S(1)} %cholesky.580), custom_call_target="Cholesky" | custom-call | tf_op jit(solution)/shard_map/jit(cholesky)/cholesky | solution.py:59
  362.4 2.5 cholesky.256
  364.9 9.8 %custom-call.59 = f32[1,128,128]{1,2,0:T(8,128)S(1)} custom-call(f32[1,128,128]{2,1,0:T(8,128)S(1)} %get-tuple-element.26), custom_call_target="InvertDiagBlocksLowerTriangular" | custom-call | tf_op jit(solution)/shard_map/jit(cholesky)/cholesky | solution.py:59
  374.8 2.4 constant_dynamic-update-slice_fusion.7
  378.7 12.1 %cholesky.245 = f32[128,128]{1,0:T(8,128)S(1)} custom-call(f32[128,128]{1,0:T(8,128)S(1)} %cholesky.584), custom_call_target="Cholesky" | custom-call | tf_op jit(solution)/shard_map/jit(cholesky)/cholesky | solution.py:59
  391.4 9.8 %custom-call.60 = f32[1,128,128]{1,2,0:T(8,128)S(1)} custom-call(f32[1,128,128]{2,1,0:T(8,128)S(1)} %get-tuple-element.23), custom_call_target="InvertDiagBlocksLowerTriangular" | custom-call | tf_op jit(solution)/shard_map/jit(cholesky)/cholesky | solution.py:59
  404.6 11.7 %cholesky.469 = f32[128,128]{1,0:T(8,128)S(1)} custom-call(f32[128,128]{1,0:T(8,128)S(1)} %cholesky.589), custom_call_target="Cholesky" | custom-call | tf_op jit(solution)/shard_map/jit(cholesky)/cholesky | solution.py:59
  417.5 9.8 %custom-call.61 = f32[1,128,128]{1,2,0:T(8,128)S(1)} custom-call(f32[1,128,128]{2,1,0:T(8,128)S(1)} %get-tuple-element.20), custom_call_target="InvertDiagBlocksLowerTriangular" | custom-call | tf_op jit(solution)/shard_map/jit(cholesky)/cholesky | solution.py:59
  430.9 11.9 %cholesky.488 = f32[128,128]{1,0:T(8,128)S(1)} custom-call(f32[128,128]{1,0:T(8,128)S(1)} %cholesky.594), custom_call_target="Cholesky" | custom-call | tf_op jit(solution)/shard_map/jit(cholesky)/cholesky | solution.py:59
  444.0 9.8 %custom-call.62 = f32[1,128,128]{1,2,0:T(8,128)S(1)} custom-call(f32[1,128,128]{2,1,0:T(8,128)S(1)} %get-tuple-element.17), custom_call_target="InvertDiagBlocksLowerTriangular" | custom-call | tf_op jit(solution)/shard_map/jit(cholesky)/cholesky | solution.py:59
  457.3 11.7 %cholesky.507 = f32[128,128]{1,0:T(8,128)S(1)} custom-call(f32[128,128]{1,0:T(8,128)S(1)} %cholesky.599), custom_call_target="Cholesky" | custom-call | tf_op jit(solution)/shard_map/jit(cholesky)/cholesky | solution.py:59
  470.3 10.0 %custom-call.63 = f32[1,128,128]{1,2,0:T(8,128)S(1)} custom-call(f32[1,128,128]{2,1,0:T(8,128)S(1)} %get-tuple-element.14), custom_call_target="InvertDiagBlocksLowerTriangular" | custom-call | tf_op jit(solution)/shard_map/jit(cholesky)/cholesky | solution.py:59
  483.6 11.7 %cholesky.527 = f32[128,128]{1,0:T(8,128)S(1)} custom-call(f32[128,128]{1,0:T(8,128)S(1)} %cholesky.604), custom_call_target="Cholesky" | custom-call | tf_op jit(solution)/shard_map/jit(cholesky)/cholesky | solution.py:59
  496.6 9.8 %custom-call.64 = f32[1,128,128]{1,2,0:T(8,128)S(1)} custom-call(f32[1,128,128]{2,1,0:T(8,128)S(1)} %get-tuple-element.11), custom_call_target="InvertDiagBlocksLowerTriangular" | custom-call | tf_op jit(solution)/shard_map/jit(cholesky)/cholesky | solution.py:59
  509.4 11.9 %cholesky.547 = f32[128,128]{1,0:T(8,128)S(1)} custom-call(f32[128,128]{1,0:T(8,128)S(1)} %cholesky.609), custom_call_target="Cholesky" | custom-call | tf_op jit(solution)/shard_map/jit(cholesky)/cholesky | solution.py:59
  522.6 9.8 %custom-call.65 = f32[1,128,128]{1,2,0:T(8,128)S(1)} custom-call(f32[1,128,128]{2,1,0:T(8,128)S(1)} %get-tuple-element.8), custom_call_target="InvertDiagBlocksLowerTriangular" | custom-call | tf_op jit(solution)/shard_map/jit(cholesky)/cholesky | solution.py:59
  535.0 11.7 %cholesky.565 = f32[128,128]{1,0:T(8,128)S(1)} custom-call(f32[128,128]{1,0:T(8,128)S(1)} %convolution_subtract_fusion.6), custom_call_target="Cholesky" | custom-call | tf_op jit(solution)/shard_map/jit(cholesky)/cholesky | solution.py:59
  (59 shorter events, 43.3 us)
Async XLA Ops:
  6.5 11.9 %copy-start = (f32[2,128,512]{2,1,0:T(8,128)S(1)}, f32[2,128,512]{2,1,0:T(8,128)}, u32[]{:S(2)}) copy-start(f32[2,128,512]{2,1,0:T(8,128)} %param.7) | copy-start | bytes 1572868
  11.1 7.3 %copy-start.3 = (s32[2,512]{1,0:T(2,128)S(1)}, s32[2,512]{1,0:T(2,128)}, u32[]{:S(2)}) copy-start(s32[2,512]{1,0:T(2,128)} %param.8) | copy-start | bytes 12292
  13.1 20.6 %all-to-all-start = ((f32[8,32,1024]{2,1,0:T(8,128)}), f32[8,32,1024]{2,1,0:T(8,128)S(1)}, u32[]{:S(2)}, u32[]{:S(2)}) async-start(f32[8,32,1024]{2,1,0:T(8,128)} %bitcast.5), calls=%async_computation | async-start | bytes 2097152 | tf_op jit(solution)/shard_map/all_to_all | solution.py:46
  18.3 310.0 %all-gather.3.cloned.1.call-start = ((), (), s32[]{:S(2)}) async-start(), calls=%async_computation.1 | async-start | bytes 20971520 | tf_op jit(solution)/shard_map/all_gather | solution.py:11
  42.0 0.7 copy-start.2
  348.8 1.9 copy-start.1
Sparse Core Ops, SparseCore 0:
  42.2 286.1 all-gather.2
